TPU v7x, 32 devices: a whole 2x2x4 slice. The times are simulated.
32 devices in a mesh: grp: 2 (over y), gy: 4 (over z), gx: 2 (over x), gz: 2 (over core).
Axes of the slice: x: 2, y: 2, z: 4, core: 2. Of those that a mesh axis runs over, the one named last changes fastest.
Arguments:
- pair: bfloat16 [1024, 512, 128], P(('grp', 'gx', 'gz'), 'gy'), parts along dimension 0, may hold values from -6 to 6
- lengths: int32 [2], P('grp'), parts along dimension 0, may hold values from 256 to 512
- ln_gain: float32 [128], replicated, may hold values from 0.1 to 1.9
- ln_bias: float32 [128], replicated, may hold values from -3 to 3
- w_ab: bfloat16 [128, 512], replicated, may hold values from -0.5 to 0.5
- w_gate: bfloat16 [128, 128], replicated, may hold values from -0.5 to 0.5
- out_gain: float32 [128], replicated, may hold values from 0.1 to 1.9
- out_bias: float32 [128], replicated, may hold values from -3 to 3
- w_out: bfloat16 [128, 128], replicated, may hold values from -0.5 to 0.5
Outputs:
- update: bfloat16 [1024, 512, 128], P(('grp', 'gx', 'gz'), 'gy'), parts along dimension 0
There are 2 independent parts, one for each index of `grp`. A program takes and returns all parts, laid end to end along the dimension named above; an argument that names none is the same for every part. Nothing has to cross between parts.
Inputs may be any that keep to these rules, and one draw needn't show every extreme that they name: Residues from lengths[0] on are padding.
All inputs are finite; a program needn't handle non-finite values.
Results may differ from a plain program's by a relative error of at most 0.0052.
Values may be sent and summed in bfloat16 or wider, within the bound.
A program may use at most 128 MiB of HBM per device.

v0:
```python
import jax
import jax.numpy as jnp
from jax import lax
from jax.sharding import PartitionSpec as P


def layer_norm(values, gain, bias):
    values = values.astype(jnp.float32)
    mean = jnp.mean(values, -1, keepdims=True)
    spread = jnp.mean(jnp.square(values - mean), -1, keepdims=True)
    return (values - mean) * lax.rsqrt(spread + 1e-05) * gain + bias


def channel_norm(values, gain, bias):
    mean = jnp.mean(values, 0, keepdims=True)
    spread = jnp.mean(jnp.square(values - mean), 0, keepdims=True)
    return (values - mean) * lax.rsqrt(spread + 1e-05) * gain[:, None, None] + bias[:, None, None]


def body(pair, lengths, ln_gain, ln_bias, w_ab, w_gate, out_gain, out_bias, w_out):
    tile_rows, tile_cols, width = pair.shape
    hidden = w_out.shape[0]
    row_start = lax.axis_index(("gx", "gz")) * tile_rows
    col_index = lax.axis_index("gy")
    col_start = col_index * tile_cols
    normed = layer_norm(pair, ln_gain, ln_bias).astype(jnp.bfloat16)
    flat = normed.reshape(tile_rows * tile_cols, width)
    proj = jnp.dot(flat, w_ab, preferred_element_type=jnp.float32).reshape(
        tile_rows, tile_cols, 4 * hidden
    )
    row_live = (row_start + jnp.arange(tile_rows, dtype=jnp.int32) < lengths[0]).astype(jnp.float32)
    col_live = (col_start + jnp.arange(tile_cols, dtype=jnp.int32) < lengths[0]).astype(jnp.float32)
    pair_mask = (row_live[:, None] * col_live[None, :])[..., None]
    left = (pair_mask * jax.nn.sigmoid(proj[..., :hidden]) * proj[..., hidden : 2 * hidden]).astype(
        jnp.bfloat16
    )
    right = (
        pair_mask * jax.nn.sigmoid(proj[..., 2 * hidden : 3 * hidden]) * proj[..., 3 * hidden :]
    ).astype(jnp.bfloat16)
    left_major = jnp.transpose(left, (2, 0, 1))
    right_major = jnp.transpose(right, (2, 0, 1))
    column_rows = lax.all_gather(right_major, ("gx", "gz"), axis=1, tiled=True)
    right_mine = lax.all_to_all(column_rows, "gy", split_axis=1, concat_axis=2, tiled=True)
    triangle = jnp.einsum(
        "cik,cjk->cij",
        lax.all_gather(left_major, "gy", axis=2, tiled=True),
        right_mine,
        preferred_element_type=jnp.float32,
    )
    tri_norm = channel_norm(triangle, out_gain, out_bias).astype(jnp.bfloat16)
    gate = jax.nn.sigmoid(jnp.dot(flat, w_gate, preferred_element_type=jnp.float32)).reshape(
        tile_rows, tile_cols, width
    )
    projected = jnp.einsum("cij,cd->ijd", tri_norm, w_out, preferred_element_type=jnp.float32)
    return (gate * projected).astype(jnp.bfloat16)


def solution(mesh):
    in_specs = (P(("grp", "gx", "gz"), "gy", None), P("grp"), P(), P(), P(), P(), P(), P(), P())
    out_specs = P(("grp", "gx", "gz"), "gy", None)
    return jax.shard_map(body, mesh=mesh, in_specs=in_specs, out_specs=out_specs, check_vma=False)
```

profile of v0, /device:TPU:0, one launch (start us, length us, event | category | flops | bytes accessed | tf_op | source)
XLA Modules:
  0.0 898.8 jit_solution(9406988459465322010)
XLA Ops:
  6.5 0.0 copy-start
  6.5 0.0 copy-start.7
  6.5 0.0 copy-start.6
  6.5 0.0 all-gather.5.cloned.1.call-start
  6.6 0.0 copy-start.3
  7.4 3.8 convert_reduce_fusion
  11.2 6.0 fusion.5
  17.2 0.1 broadcast_multiply_fusion
  17.3 0.0 copy-done.7
  17.3 0.0 copy-done.6
  17.3 0.0 copy-done.3
  17.4 4.9 fusion.8
  22.3 0.0 copy-done
  22.3 0.0 copy-start.4
  22.3 13.1 %fusion.25 = f32[128,128,512]{2,1,0:T(8,128)} fusion(bf16[128,128,128]{2,1,0:T(8,128)(2,1)S(1)} %fusion.8, bf16[128,512]{1,0:T(8,128)(2,1)S(1)} %copy-done), kind=kOutput, calls=%fused_computation.34 | convolution fusion | flops 2147483648 | bytes 37879808 | tf_op jit(solution)/shard_map/dot_general | solution.py:28
  35.5 0.0 copy-done.4
  35.5 15.6 %fusion.22 = (bf16[128,128,128]{0,2,1:T(8,128)(2,1)}, bf16[128,128,128]{0,2,1:T(8,128)(2,1)}) fusion(f32[128,128,512]{2,1,0:T(8,128)} %fusion.25, f32[128,128]{1,0:T(8,128)S(1)} %broadcast_multiply_fusion), kind=kLoop, calls=%fused_computation.33 | loop fusion | flops 25165824 | bytes 42008576 | tf_op jit(solution)/shard_map/transpose | solution.py:41
  51.1 6.4 copy.13
  57.4 0.0 all-gather.5.cloned.1.call-update
  57.5 0.0 all-gather.3.cloned.1.call-start
  57.5 0.7 all-gather.3.cloned.1.call-update
  58.2 0.0 copy-start.10
  58.2 108.0 %all-gather.5.cloned.1.call-done = bf16[128,512,128]{2,0,1:T(8,128)(2,1)} async-done(((bf16[128,128,128]{2,0,1:T(8,128)(2,1)}), bf16[128,512,128]{2,0,1:T(8,128)(2,1)}) %all-gather.5.cloned.1.call-update) | async-done | bytes 16777232 | tf_op jit(solution)/shard_map/all_gather | solution.py:42
  166.2 7.3 all-to-all-start
  173.5 0.0 copy-done.10
  173.5 9.0 %fusion.2 = f32[16384,128]{1,0:T(8,128)} fusion(bf16[16384,128]{1,0:T(8,128)(2,1)} %bitcast.24, bf16[128,128]{1,0:T(8,128)(2,1)S(1)} %copy-done.10), kind=kOutput, calls=%fused_computation.3 | convolution fusion | flops 543162368 | bytes 12615680 | tf_op jit(solution)/shard_map/dot_general | solution.py:51
  182.5 580.3 %all-gather.3.cloned.1.call-done = bf16[128,128,512]{0,2,1:T(8,128)(2,1)} async-done(((bf16[128,128,128]{0,2,1:T(8,128)(2,1)}), bf16[128,128,512]{0,2,1:T(8,128)(2,1)}) %all-gather.3.cloned.1.call-update) | async-done | bytes 16777232 | tf_op jit(solution)/shard_map/all_gather | solution.py:46
  762.8 23.4 %copy.15 = bf16[128,128,512]{2,1,0:T(8,128)(2,1)} copy(bf16[128,128,512]{0,2,1:T(8,128)(2,1)} %all-gather.3.cloned.1.call-done) | data formatting | bytes 33554432 | tf_op jit(solution)/shard_map/all_gather | solution.py:46
  786.2 20.3 %all-to-all-done = bf16[128,512,128]{2,0,1:T(8,128)(2,1)} async-done(((bf16[128,512,128]{2,0,1:T(8,128)(2,1)}), bf16[128,512,128]{2,0,1:T(8,128)(2,1)}, u32[]{:S(2)}, u32[]{:S(2)}) %all-to-all-start) | async-done | bytes 16777248 | tf_op jit(solution)/shard_map/all_to_all | solution.py:43
  806.5 22.0 %copy.22 = bf16[128,4,128,128]{3,1,2,0:T(4,128)(2,1)} copy(bf16[128,4,128,128]{3,0,2,1:T(8,128)(2,1)} %bitcast.6) | data formatting | bytes 33554432 | tf_op jit(solution)/shard_map/all_to_all | solution.py:43
  828.6 24.9 %all_to_all.16 = bf16[128,128,512]{2,1,0:T(8,128)(2,1)} reshape(bf16[128,128,4,128]{3,2,1,0:T(4,128)(2,1)} %bitcast.23) | data formatting | bytes 33554432 | tf_op jit(solution)/shard_map/all_to_all | solution.py:43
  853.4 16.4 %fusion.28 = (f32[128,128]{1,0:T(8,128)S(1)}, f32[128,128,128]{2,1,0:T(8,128)}) fusion(bf16[128,128,512]{2,1,0:T(8,128)(2,1)} %copy.15, bf16[128,128,512]{2,1,0:T(8,128)(2,1)} %all_to_all.16), kind=kOutput, calls=%fused_computation.44 | convolution fusion | flops 2149564416 | bytes 42008576 | tf_op jit(solution)/shard_map/cik,cjk->cij/dot_general | solution.py:44
  869.8 0.0 copy-start.2
  869.8 0.0 copy-start.8
  869.8 0.0 copy-start.9
  869.8 4.4 multiply_reduce_fusion
  874.2 0.0 copy-start.5
  874.3 1.3 copy-done.2
  875.6 0.0 copy-done.8
  875.6 0.0 copy-done.9
  875.6 2.0 add_convert_fusion
  877.6 0.0 copy-start.1
  877.6 0.0 copy-done.5
  877.6 14.4 %multiply_convert_fusion = bf16[128,128,128]{2,1,0:T(8,128)(2,1)} fusion(f32[128,128,128]{2,1,0:T(8,128)} %bitcast.25, bf16[128,128,128]{2,1,0:T(8,128)(2,1)S(1)} %add_convert_fusion, bf16[128,128]{1,0:T(8,128)(2,1)S(1)} %copy-done.5), kind=kOutput, calls=%fused_computation.27 | convolution fusion | flops 541065216 | bytes 16809984 | tf_op jit(solution)/shard_map/cij,cd->ijd/dot_general | solution.py:54
  891.9 0.0 copy-done.1
  (5 shorter events, 0.1 us)
Async XLA Ops:
  6.5 15.8 %copy-start = (bf16[128,512]{1,0:T(8,128)(2,1)S(1)}, bf16[128,512]{1,0:T(8,128)(2,1)}, u32[]{:S(2)}) copy-start(bf16[128,512]{1,0:T(8,128)(2,1)} %param.13) | copy-start | bytes 393220
  6.5 10.8 %copy-start.7 = (f32[128]{0:T(128)S(1)}, f32[128]{0:T(128)}, u32[]{:S(2)}) copy-start(f32[128]{0:T(128)} %param.11) | copy-start | bytes 1540
  6.5 10.8 %copy-start.6 = (f32[128]{0:T(128)S(1)}, f32[128]{0:T(128)}, u32[]{:S(2)}) copy-start(f32[128]{0:T(128)} %param.12) | copy-start | bytes 1540
  6.5 159.7 %all-gather.5.cloned.1.call-start = ((), (), s32[]{:S(2)}) async-start(), calls=%async_computation.2 | async-start | bytes 20971520 | tf_op jit(solution)/shard_map/all_gather | solution.py:42
  6.6 10.8 %copy-start.3 = (bf16[128,128,128]{2,1,0:T(8,128)(2,1)S(1)}, bf16[128,128,128]{2,1,0:T(8,128)(2,1)}, u32[]{:S(2)}) copy-start(bf16[128,128,128]{2,1,0:T(8,128)(2,1)} %param.9) | copy-start | bytes 12582916
  22.3 13.2 %copy-start.4 = (bf16[128,128,128]{2,1,0:T(8,128)(2,1)}, bf16[128,128,128]{2,1,0:T(8,128)(2,1)S(1)}, u32[]{:S(2)}) copy-start(bf16[128,128,128]{2,1,0:T(8,128)(2,1)S(1)} %fusion.8) | copy-start | bytes 12582916
  57.5 705.3 %all-gather.3.cloned.1.call-start = ((), (), s32[]{:S(2)}) async-start(), calls=%async_computation.1 | async-start | bytes 20971520 | tf_op jit(solution)/shard_map/all_gather | solution.py:46
  58.2 115.3 %copy-start.10 = (bf16[128,128]{1,0:T(8,128)(2,1)S(1)}, bf16[128,128]{1,0:T(8,128)(2,1)}, u32[]{:S(2)}) copy-start(bf16[128,128]{1,0:T(8,128)(2,1)} %param.14) | copy-start | bytes 98308
  166.2 640.3 %all-to-all-start = ((bf16[128,512,128]{2,0,1:T(8,128)(2,1)}), bf16[128,512,128]{2,0,1:T(8,128)(2,1)}, u32[]{:S(2)}, u32[]{:S(2)}) async-start(bf16[128,512,128]{2,0,1:T(8,128)(2,1)} %all-gather.5.cloned.1.call-done), calls=%async_computation | async-start | bytes 33554432 | tf_op jit(solution)/shard_map/all_to_all | solution.py:43
  869.8 5.8 copy-start.2
  869.8 5.8 copy-start.8
  869.8 5.8 copy-start.9
  874.2 3.3 copy-start.5
  877.6 14.4 %copy-start.1 = (bf16[128,512]{1,0:T(8,128)(2,1)S(1)}, bf16[128,512]{1,0:T(8,128)(2,1)}, u32[]{:S(2)}) copy-start(bf16[128,512]{1,0:T(8,128)(2,1)} %param.13) | copy-start | bytes 393220
Sparse Core Ops, SparseCore 0:
  57.6 108.6 all-gather.4
  167.8 594.9 all-gather.2
where the time goes:
time: 900 us; the launch traced here: 899 us
  waiting for transfers between devices  709 us (79%)
  local copies, waits for them, and re-layouts  78 us (9%)
  matrix products  52.9 us (6%)
  other arithmetic  36.9 us (4%)
  between operations  14.4 us (2%)
    all_gather x1, waiting for transfers between devices, body(): lax.all_gather(left_major, 'gy', axis=2, tiled=True)  580 us
    all_gather x1, waiting for transfers between devices, body(): column_rows = lax.all_gather(right_major, ('gx', 'gz'), axis=1, tiled=True)  108 us
    all_to_all x2, local copies, waits for them, and re-layouts, body(): lax.all_to_all(column_rows, 'gy', split_axis=1, concat_axis=2, tiled=True)  46.9 us
    all_gather x1, local copies, waits for them, and re-layouts, body(): lax.all_gather(left_major, 'gy', axis=2, tiled=True)  23.4 us
    all_to_all x1, waiting for transfers between devices, body(): lax.all_to_all(column_rows, 'gy', split_axis=1, concat_axis=2, tiled=True)  20.3 us
  transfers between devices with their start and end apart: 3, of which 3 were waited for; matrix products, arithmetic and copies ran while one was open for 4% of the time, Pallas kernels for 0%

commit v1 on v0

--- a/solution.py
+++ b/solution.py
@@ -40,7 +40,10 @@
     left_major = jnp.transpose(left, (2, 0, 1))
     right_major = jnp.transpose(right, (2, 0, 1))
     column_rows = lax.all_gather(right_major, ("gx", "gz"), axis=1, tiled=True)
-    right_mine = lax.all_to_all(column_rows, "gy", split_axis=1, concat_axis=2, tiled=True)
+    size = lax.axis_size("gy")
+    tiles = jnp.stack(jnp.split(column_rows, size, axis=1), axis=0)
+    tiles = lax.all_to_all(tiles, "gy", split_axis=0, concat_axis=0)
+    right_mine = jnp.concatenate(tiles, axis=2)
     triangle = jnp.einsum(
         "cik,cjk->cij",
         lax.all_gather(left_major, "gy", axis=2, tiled=True),

time: 900 us -> 863 us (0.959)
  waiting for transfers between devices: 709 us -> 677 us
    all_gather x1, waiting for transfers between devices: 580 us -> 536 us  [body(): lax.all_gather(left_major, 'gy', axis=2, tiled=True)]
    all_to_all x2 -> x1, local copies, waits for them, and re-layouts: 46.9 us -> 14.1 us  [body(): tiles = lax.all_to_all(tiles, 'gy', split_axis=0, concat_axis=0)]
    another operation x0 -> x2, local copies, waits for them, and re-layouts: none -> 32 us  [body(): tiles = jnp.stack(jnp.split(column_rows, size, axis=1), axis=0)]
    all_to_all x1, waiting for transfers between devices: 20.3 us -> 32.7 us  [body(): tiles = lax.all_to_all(tiles, 'gy', split_axis=0, concat_axis=0)]
  transfers between devices with their start and end apart: 3 -> 3, of which waited for: 3 -> 3; matrix products, arithmetic and copies ran while one was open for 4% -> 8% of each run, Pallas kernels for 0% -> 0%
where the time goes in v1:
time: 863 us; the launch traced here: 862 us
  waiting for transfers between devices  677 us (78%)
  local copies, waits for them, and re-layouts  76.7 us (9%)
  matrix products  44.5 us (5%)
  other arithmetic  41.3 us (5%)
  between operations  14.4 us (2%)
    all_gather x1, waiting for transfers between devices, body(): lax.all_gather(left_major, 'gy', axis=2, tiled=True)  536 us
    all_gather x1, waiting for transfers between devices, body(): column_rows = lax.all_gather(right_major, ('gx', 'gz'), axis=1, tiled=True)  108 us
    all_to_all x1, waiting for transfers between devices, body(): tiles = lax.all_to_all(tiles, 'gy', split_axis=0, concat_axis=0)  32.7 us
    another operation x2, local copies, waits for them, and re-layouts, body(): tiles = jnp.stack(jnp.split(column_rows, size, axis=1), axis=0)  32 us
    all_gather x1, local copies, waits for them, and re-layouts, body(): lax.all_gather(left_major, 'gy', axis=2, tiled=True)  23.5 us
  transfers between devices with their start and end apart: 3, of which 3 were waited for; matrix products, arithmetic and copies ran while one was open for 8% of the time, Pallas kernels for 0%

profile of v1, /device:TPU:0, one launch (start us, length us, event | category | flops | bytes accessed | tf_op | source)
XLA Modules:
  0.0 861.7 jit_solution(16768042044538117121)
XLA Ops:
  6.5 0.0 copy-start
  6.5 0.0 copy-start.6
  6.5 0.0 copy-start.5
  6.5 0.0 all-gather.5.cloned.1.call-start
  6.6 0.0 copy-start.2
  7.4 3.8 convert_reduce_fusion
  11.2 6.0 fusion.5
  17.2 0.1 broadcast_multiply_fusion
  17.3 0.0 copy-done.6
  17.3 0.0 copy-done.5
  17.3 0.0 copy-done.2
  17.4 4.9 fusion.8
  22.3 0.0 copy-done
  22.3 0.0 copy-start.3
  22.3 13.1 %fusion.25 = f32[128,128,512]{2,1,0:T(8,128)} fusion(bf16[128,128,128]{2,1,0:T(8,128)(2,1)S(1)} %fusion.8, bf16[128,512]{1,0:T(8,128)(2,1)S(1)} %copy-done), kind=kOutput, calls=%fused_computation.38 | convolution fusion | flops 2147483648 | bytes 37879808 | tf_op jit(solution)/shard_map/dot_general | solution.py:28
  35.5 0.0 copy-done.3
  35.5 15.5 %fusion.22 = (bf16[128,128,128]{0,2,1:T(8,128)(2,1)}, bf16[128,128,128]{0,2,1:T(8,128)(2,1)}) fusion(f32[128,128,512]{2,1,0:T(8,128)} %fusion.25, f32[128,128]{1,0:T(8,128)S(1)} %broadcast_multiply_fusion), kind=kLoop, calls=%fused_computation.37 | loop fusion | flops 25165824 | bytes 42008576 | tf_op jit(solution)/shard_map/transpose | solution.py:41
  51.0 6.4 copy.24
  57.4 0.0 all-gather.5.cloned.1.call-update
  57.4 0.0 all-gather.3.cloned.1.call-start
  57.5 0.7 all-gather.3.cloned.1.call-update
  58.2 108.0 %all-gather.5.cloned.1.call-done = bf16[128,512,128]{2,0,1:T(8,128)(2,1)} async-done(((bf16[128,128,128]{2,0,1:T(8,128)(2,1)}), bf16[128,512,128]{2,0,1:T(8,128)(2,1)}) %all-gather.5.cloned.1.call-update) | async-done | bytes 16777232 | tf_op jit(solution)/shard_map/all_gather | solution.py:42
  166.2 7.8 slice_bitcast_fusion.3
  174.0 8.0 pad_maximum_fusion
  181.9 24.2 %copy.25 = bf16[4,128,128,128]{2,3,1,0:T(8,128)(2,1)} copy(bf16[4,128,128,128]{3,1,2,0:T(8,128)(2,1)} %pad_maximum_fusion) | data formatting | bytes 33554432 | tf_op jit(solution)/shard_map/stack | solution.py:44
  206.1 0.0 copy-start.9
  206.1 7.3 all-to-all-start
  213.4 0.0 copy-done.9
  213.4 7.8 fusion.2
  221.2 536.0 %all-gather.3.cloned.1.call-done = bf16[128,128,512]{0,2,1:T(8,128)(2,1)} async-done(((bf16[128,128,128]{0,2,1:T(8,128)(2,1)}), bf16[128,128,512]{0,2,1:T(8,128)(2,1)}) %all-gather.3.cloned.1.call-update) | async-done | bytes 16777232 | tf_op jit(solution)/shard_map/all_gather | solution.py:49
  757.2 23.5 %copy.27 = bf16[128,128,512]{2,1,0:T(8,128)(2,1)} copy(bf16[128,128,512]{0,2,1:T(8,128)(2,1)} %all-gather.3.cloned.1.call-done) | data formatting | bytes 33554432 | tf_op jit(solution)/shard_map/all_gather | solution.py:49
  780.7 32.7 %all-to-all-done = bf16[4,128,128,128]{2,3,1,0:T(8,128)(2,1)} async-done(((bf16[4,128,128,128]{2,3,1,0:T(8,128)(2,1)}), bf16[4,128,128,128]{2,3,1,0:T(8,128)(2,1)}, u32[]{:S(2)}, u32[]{:S(2)}) %all-to-all-start) | async-done | bytes 16777248 | tf_op jit(solution)/shard_map/all_to_all | solution.py:45
  813.4 14.1 %copy.26 = bf16[4,128,128,128]{2,3,0,1:T(8,128)(2,1)} copy(bf16[4,128,128,128]{2,3,1,0:T(8,128)(2,1)} %all-to-all-done) | data formatting | bytes 33554432 | tf_op jit(solution)/shard_map/all_to_all | solution.py:45
  827.5 12.9 %fusion.28 = (f32[128,128]{1,0:T(8,128)S(1)}, f32[128,128,128]{2,1,0:T(8,128)S(1)}) fusion(bf16[128,128,512]{2,1,0:T(8,128)(2,1)} %copy.27, bf16[128,128,512]{1,2,0:T(8,128)(2,1)} %bitcast.30), kind=kOutput, calls=%fused_computation.48 | convolution fusion | flops 2149564416 | bytes 42008576 | tf_op jit(solution)/shard_map/cik,cjk->cij/dot_general | solution.py:47
  840.4 0.0 copy-start.7
  840.4 0.0 copy-start.8
  840.4 0.0 slice-start
  840.4 0.9 multiply_reduce_fusion
  841.4 0.0 copy-done.7
  841.4 0.0 copy-done.8
  841.4 0.0 slice-start.1
  841.4 2.0 add_convert_fusion
  843.4 0.0 copy-start.1
  843.4 0.0 slice-done
  843.4 0.0 copy-done.4
  843.4 0.7 slice-done.1
  844.1 10.7 %multiply_convert_fusion = bf16[128,128,128]{2,1,0:T(8,128)(2,1)} fusion(f32[128,128,128]{2,1,0:T(8,128)S(1)} %bitcast.34, bf16[128,128,128]{2,1,0:T(8,128)(2,1)S(1)} %add_convert_fusion, bf16[128,128]{1,0:T(8,128)(2,1)S(1)} %copy-done.4), kind=kOutput, calls=%fused_computation.27 | convolution fusion | flops 541065216 | bytes 16809984 | tf_op jit(solution)/shard_map/cij,cd->ijd/dot_general | solution.py:57
  854.9 0.0 copy-done.1
  (7 shorter events, 0.1 us)
Async XLA Ops:
  6.5 15.8 %copy-start = (bf16[128,512]{1,0:T(8,128)(2,1)S(1)}, bf16[128,512]{1,0:T(8,128)(2,1)}, u32[]{:S(2)}) copy-start(bf16[128,512]{1,0:T(8,128)(2,1)} %param.13) | copy-start | bytes 393220
  6.5 10.8 %copy-start.6 = (f32[128]{0:T(128)S(1)}, f32[128]{0:T(128)}, u32[]{:S(2)}) copy-start(f32[128]{0:T(128)} %param.11) | copy-start | bytes 1540
  6.5 10.8 %copy-start.5 = (f32[128]{0:T(128)S(1)}, f32[128]{0:T(128)}, u32[]{:S(2)}) copy-start(f32[128]{0:T(128)} %param.12) | copy-start | bytes 1540
  6.5 159.6 %all-gather.5.cloned.1.call-start = ((), (), s32[]{:S(2)}) async-start(), calls=%async_computation.2 | async-start | bytes 20971520 | tf_op jit(solution)/shard_map/all_gather | solution.py:42
  6.6 10.8 %copy-start.2 = (bf16[128,128,128]{2,1,0:T(8,128)(2,1)S(1)}, bf16[128,128,128]{2,1,0:T(8,128)(2,1)}, u32[]{:S(2)}) copy-start(bf16[128,128,128]{2,1,0:T(8,128)(2,1)} %param.9) | copy-start | bytes 12582916
  22.3 13.1 %copy-start.3 = (bf16[128,128,128]{2,1,0:T(8,128)(2,1)}, bf16[128,128,128]{2,1,0:T(8,128)(2,1)S(1)}, u32[]{:S(2)}) copy-start(bf16[128,128,128]{2,1,0:T(8,128)(2,1)S(1)} %fusion.8) | copy-start | bytes 12582916
  57.4 699.8 %all-gather.3.cloned.1.call-start = ((), (), s32[]{:S(2)}) async-start(), calls=%async_computation.1 | async-start | bytes 20971520 | tf_op jit(solution)/shard_map/all_gather | solution.py:49
  206.1 7.3 copy-start.9
  206.1 607.3 %all-to-all-start = ((bf16[4,128,128,128]{2,3,1,0:T(8,128)(2,1)}), bf16[4,128,128,128]{2,3,1,0:T(8,128)(2,1)}, u32[]{:S(2)}, u32[]{:S(2)}) async-start(bf16[4,128,128,128]{2,3,1,0:T(8,128)(2,1)} %copy.25), calls=%async_computation | async-start | bytes 33554432 | tf_op jit(solution)/shard_map/all_to_all | solution.py:45
  840.4 1.0 copy-start.7
  840.4 1.0 copy-start.8
  840.4 3.0 slice-start
  841.3 2.1 copy-start.4
  841.4 2.8 slice-start.1
  843.4 11.4 %copy-start.1 = (bf16[128,512]{1,0:T(8,128)(2,1)S(1)}, bf16[128,512]{1,0:T(8,128)(2,1)}, u32[]{:S(2)}) copy-start(bf16[128,512]{1,0:T(8,128)(2,1)} %param.13) | copy-start | bytes 393220
Sparse Core Ops, SparseCore 0:
  57.5 108.6 all-gather.4
  167.7 589.4 all-gather.2
